TPU v7x, 32 devices: a whole 2x2x4 slice. The times are simulated.
32 devices in a mesh: data: 32 (over z, y, x, core).
Axes of the slice: x: 2, y: 2, z: 4, core: 2. Of those that a mesh axis runs over, the one named last changes fastest.
Arguments:
- tokens: bfloat16 [65536, 1280], P('data')
- w_up: bfloat16 [1280, 5120], replicated
- w_down: bfloat16 [5120, 1280], replicated
- heads: bfloat16 [8, 1280, 2], replicated
- labels: int32 [8, 65536], P(None, 'data')
Outputs:
- output 1: float32 [8], replicated
- output 2: float32 [1280, 5120], P('data')
- output 3: float32 [5120, 1280], P('data')
All inputs are finite; a program needn't handle non-finite values.
Results may differ from a plain program's by a relative error of at most 0.00256343.
Values are sent between devices in bfloat16 or wider.
A program may use at most 1 GiB of HBM per device.

v0:
```python
import jax
import jax.numpy as jnp
from jax import lax
from jax.sharding import PartitionSpec as P

SOLVER_STEPS = 20
EXACT_PREC = lax.Precision.HIGHEST


def solve_weights(full_gram):
    num_tasks = full_gram.shape[0]
    step_scale = jnp.trace(full_gram) / num_tasks

    def update(step_idx, mix_wts):
        descent = jnp.sum(full_gram * mix_wts[None, :], axis=1)
        mix_wts = mix_wts * jnp.exp(-descent / step_scale)
        return mix_wts / jnp.sum(mix_wts)

    uniform_start = jnp.full((num_tasks,), 1.0 / num_tasks, jnp.float32)
    return lax.fori_loop(0, SOLVER_STEPS, update, uniform_start)


def solution(mesh):
    group_size = mesh.shape['data']

    def local_step(tok_rows, w_up, w_down, heads, label_rows):
        total_rows = tok_rows.shape[0] * group_size
        num_classes = heads.shape[2]
        pre_act = jnp.dot(tok_rows, w_up, preferred_element_type=jnp.float32).astype(jnp.bfloat16)
        hidden = jax.nn.gelu(pre_act.astype(jnp.float32)).astype(jnp.bfloat16)
        trunk_out = tok_rows.astype(jnp.float32) + jnp.dot(hidden, w_down, preferred_element_type=jnp.float32)
        logits = jnp.einsum('bd,tdc->tbc', trunk_out.astype(jnp.bfloat16), heads, preferred_element_type=jnp.float32)
        onehot = (label_rows[:, :, None] == jnp.arange(num_classes)[None, None, :]).astype(jnp.float32)
        task_resid = (jax.nn.softmax(logits, axis=-1) - onehot) / total_rows
        heads_f32 = heads.astype(jnp.float32)
        head_gram = jnp.einsum('tdc,sde->tcse', heads_f32, heads_f32, precision=EXACT_PREC)
        res_outer = jnp.einsum('tbc,sbe->tcse', task_resid, task_resid, precision=EXACT_PREC)
        part_gram = jnp.sum(res_outer * head_gram, axis=(1, 3))
        full_gram = lax.psum(part_gram, 'data')
        mix_wts = solve_weights(full_gram)
        d_out = jnp.einsum('tbc,tdc->bd', task_resid * mix_wts[:, None, None], heads_f32, precision=EXACT_PREC).astype(jnp.bfloat16)
        grad_down = lax.dot_general(hidden, d_out, (((0,), (0,)), ((), ())), preferred_element_type=jnp.float32)
        d_hidden = lax.dot_general(d_out, w_down, (((1,), (1,)), ((), ())), preferred_element_type=jnp.float32)
        gelu_vjp = jax.vjp(jax.nn.gelu, pre_act.astype(jnp.float32))[1]
        d_pre = gelu_vjp(d_hidden)[0].astype(jnp.bfloat16)
        grad_up = lax.dot_general(tok_rows, d_pre, (((0,), (0,)), ((), ())), preferred_element_type=jnp.float32)
        up_shard = lax.psum_scatter(grad_up, 'data', scatter_dimension=0, tiled=True)
        down_shard = lax.psum_scatter(grad_down, 'data', scatter_dimension=0, tiled=True)
        return mix_wts, up_shard, down_shard

    return jax.shard_map(local_step, mesh=mesh, in_specs=(P('data', None), P(), P(), P(), P(None, 'data')), out_specs=(P(), P('data', None), P('data', None)), check_vma=False)
```

profile of v0, /device:TPU:0, one launch (start us, length us, event | category | flops | bytes accessed | tf_op | source)
XLA Modules:
  0.0 780.7 jit_solution(17961479052626585362)
XLA Ops:
  7.2 33.9 %convolution_convert_fusion = bf16[2048,5120]{1,0:T(8,128)(2,1)} fusion(bf16[2048,1280]{1,0:T(8,128)(2,1)} %param.7, bf16[1280,5120]{1,0:T(8,128)(2,1)} %param.8), kind=kOutput, calls=%fused_computation.20 | convolution fusion | flops 26854031360 | bytes 39321600 | tf_op jit(solution)/shard_map/dot_general | solution.py:29
  41.2 46.8 %fusion.37 = (f32[8,2048]{1,0:T(8,128)S(1)}, f32[8,2048,2]{1,0,2:T(8,128)S(1)}) fusion(bf16[8,1280,2]{1,2,0:T(2,128)(2,1)S(1)} %copy-done.2, bf16[5120,1280]{1,0:T(8,128)(2,1)} %param.9, bf16[2048,1280]{1,0:T(8,128)(2,1)} %param.7, bf16[2048,5120]{1,0:T(8,128)(2,1)} %convolution_convert_fusion), kind=kOutput, calls=%fused_computation.55 | convolution fusion | flops 27040169984 | bytes 39559168 | tf_op jit(solution)/shard_map/bd,tdc->tbc/dot_general | solution.py:32
  88.1 1.0 fusion.12
  89.1 0.2 fusion.11
  89.3 42.0 %psum.7 = f32[8,8]{1,0:T(8,128)S(1)} all-reduce(f32[8,8]{1,0:T(8,128)S(1)} %fusion.11), channel_id=1, replica_groups=mesh['data'=32] {'data'}, use_global_device_ids=true, to_apply=%region_3.0 | all-reduce | flops 64 | bytes 512 | tf_op jit(solution)/shard_map/psum | solution.py:39
  131.2 0.6 select_reduce_fusion
  132.5 28.4 %while.11 = (s32[]{:T(128)}, f32[8]{0:T(128)S(1)}, f32[8,8]{1,0:T(8,128)S(1)}, f32[]{:T(128)}, s32[]{:T(128)}, /*index=5*/s32[]{:T(128)}) while((s32[]{:T(128)}, f32[8]{0:T(128)S(1)}, f32[8,8]{1,0:T(8,128)S(1)}, f32[]{:T(128)}, s32[]{:T(128)}, /*index=5*/s32[]{:T(128)}) %tuple.39), condition=%wide.region_8.9_spmd.clone, body=%wide.region_5.8_spmd.clone.sunk | while | flops 178 | bytes 636 | solution.py:20
  132.5 0.1 multiply_reduce_fusion.2
  132.6 0.6 fusion.56
  133.3 0.6 broadcast_divide_fusion.2
  134.0 0.1 multiply_reduce_fusion.2
  134.1 0.6 fusion.56
  134.7 0.6 broadcast_divide_fusion.2
  135.4 0.1 multiply_reduce_fusion.2
  135.5 0.6 fusion.56
  136.1 0.6 broadcast_divide_fusion.2
  136.8 0.1 multiply_reduce_fusion.2
  136.9 0.6 fusion.56
  137.5 0.6 broadcast_divide_fusion.2
  138.2 0.1 multiply_reduce_fusion.2
  138.3 0.6 fusion.56
  138.9 0.6 broadcast_divide_fusion.2
  139.6 0.1 multiply_reduce_fusion.2
  139.7 0.6 fusion.56
  140.4 0.6 broadcast_divide_fusion.2
  141.0 0.1 multiply_reduce_fusion.2
  141.2 0.6 fusion.56
  141.8 0.6 broadcast_divide_fusion.2
  142.5 0.1 multiply_reduce_fusion.2
  142.6 0.6 fusion.56
  143.2 0.6 broadcast_divide_fusion.2
  143.9 0.1 multiply_reduce_fusion.2
  144.0 0.6 fusion.56
  144.6 0.6 broadcast_divide_fusion.2
  145.4 0.6 fusion.56
  146.0 0.6 broadcast_divide_fusion.2
  146.8 0.6 fusion.56
  147.5 0.6 broadcast_divide_fusion.2
  148.3 0.6 fusion.56
  148.9 0.6 broadcast_divide_fusion.2
  149.7 0.6 fusion.56
  150.3 0.6 broadcast_divide_fusion.2
  151.1 0.6 fusion.56
  151.7 0.6 broadcast_divide_fusion.2
  152.5 0.6 fusion.56
  153.1 0.6 broadcast_divide_fusion.2
  153.9 0.6 fusion.56
  154.5 0.6 broadcast_divide_fusion.2
  155.3 0.6 fusion.56
  156.0 0.6 broadcast_divide_fusion.2
  156.8 0.6 fusion.56
  157.4 0.6 broadcast_divide_fusion.2
  158.2 0.6 fusion.56
  158.8 0.6 broadcast_divide_fusion.2
  159.6 0.6 fusion.56
  160.2 0.6 broadcast_divide_fusion.2
  160.9 4.7 bitcast_convert_fusion
  165.6 2.4 copy-done
  168.0 39.0 %fusion.32 = f32[5120,1280]{1,0:T(8,128)} fusion(bf16[2048,1280]{1,0:T(8,128)(2,1)S(1)} %bitcast_convert_fusion, bf16[2048,5120]{1,0:T(8,128)(2,1)} %convolution_convert_fusion), kind=kOutput, calls=%fused_computation.53 | convolution fusion | flops 26948403200 | bytes 52428800 | tf_op jit(solution)/shard_map/dot_general | solution.py:42
  207.1 60.1 %fusion.3.clone.4 = bf16[2048,5120]{1,0:T(8,128)(2,1)} fusion(bf16[2048,5120]{1,0:T(8,128)(2,1)} %convolution_convert_fusion, bf16[2048,1280]{1,0:T(8,128)(2,1)} %copy-done, bf16[5120,1280]{1,0:T(8,128)(2,1)} %param.9), kind=kOutput, calls=%fused_computation.12.clone.clone.clone.1 | convolution fusion | flops 27063746560 | bytes 60293120 | tf_op jit(solution)/shard_map/dot_general | solution.py:43
  267.1 33.2 %convolution_bitcast_fusion = f32[1280,5120]{0,1:T(8,128)} fusion(bf16[2048,1280]{1,0:T(8,128)(2,1)S(1)} %copy-done.5, bf16[2048,5120]{1,0:T(8,128)(2,1)} %fusion.3.clone.4), kind=kOutput, calls=%fused_computation.19 | convolution fusion | flops 26843545600 | bytes 52428800 | tf_op jit(solution)/shard_map/dot_general | solution.py:46
  300.4 27.3 %copy.22 = f32[1280,5120]{1,0:T(8,128)} copy(f32[1280,5120]{0,1:T(8,128)} %convolution_bitcast_fusion) | data formatting | bytes 52428800
  327.7 157.8 %reduce-scatter.5.cloned.1.call-done = f32[160,1280]{1,0:T(8,128)} async-done(((f32[5120,1280]{1,0:T(8,128)}), f32[160,1280]{1,0:T(8,128)}) %reduce-scatter.5.cloned.1.call-update) | async-done | bytes 819216 | tf_op jit(solution)/shard_map/reduce_scatter | solution.py:48
  485.5 288.2 %reduce-scatter.7.cloned.1.call-done = f32[40,5120]{1,0:T(8,128)} async-done(((f32[1280,5120]{1,0:T(8,128)}), f32[40,5120]{1,0:T(8,128)}) %reduce-scatter.7.cloned.1.call-update) | async-done | bytes 819216
  (50 shorter events, 1.6 us)
Async XLA Ops:
  7.2 478.4 %reduce-scatter.5.cloned.1.call-start = ((), (), s32[]{:S(2)}) async-start(), calls=%async_computation.2 | async-start | bytes 27033600 | tf_op jit(solution)/shard_map/reduce_scatter | solution.py:48
  7.2 33.9 %copy-start.2 = (bf16[8,1280,2]{1,2,0:T(2,128)(2,1)S(1)}, bf16[8,1280,2]{1,2,0:T(2,128)(2,1)}, u32[]{:S(2)}) copy-start(bf16[8,1280,2]{1,2,0:T(2,128)(2,1)} %param.10) | copy-start | bytes 122884
  41.1 46.9 %copy-start.1 = (s32[8,2048]{1,0:T(8,128)S(1)}, s32[8,2048]{1,0:T(8,128)}, u32[]{:S(2)}) copy-start(s32[8,2048]{1,0:T(8,128)} %param.11) | copy-start | bytes 196612
  41.2 91.3 %copy-start.3 = (f32[8]{0:T(128)S(1)}, f32[8]{0:T(128)}, u32[]{:S(2)}) copy-start(f32[8]{0:T(128)} %custom-call) | copy-start | bytes 100
  160.9 46.1 %copy-start.4 = (f32[8]{0:T(128)}, f32[8]{0:T(128)S(1)}, u32[]{:S(2)}) copy-start(f32[8]{0:T(128)S(1)} %get-tuple-element.44) | copy-start | bytes 100
  165.6 2.4 copy-start
  207.0 566.7 %reduce-scatter.7.cloned.1.call-start = ((), (), s32[]{:S(2)}) async-start(), calls=%async_computation.3 | async-start | bytes 27033600
  207.1 60.1 %copy-start.5 = (bf16[2048,1280]{1,0:T(8,128)(2,1)S(1)}, bf16[2048,1280]{1,0:T(8,128)(2,1)}, u32[]{:S(2)}) copy-start(bf16[2048,1280]{1,0:T(8,128)(2,1)} %param.7) | copy-start | bytes 15728644
Sparse Core Ops, SparseCore 0:
  207.1 278.3 reduce-scatter.4
  488.4 285.2 reduce-scatter.6
where the time goes:
time: 791 us; the launch traced here: 781 us
  waiting for transfers between devices  446 us (56%)
  matrix products  219 us (28%)
  blocking collectives  42 us (5%)
  local copies, waits for them, and re-layouts  29.7 us (4%)
  other arithmetic  28.4 us (4%)
  between operations  15 us (2%)
    unnamed x3, waiting for transfers between devices  288 us
    reduce_scatter x1, waiting for transfers between devices, local_step(): lax.psum_scatter(grad_down, 'data', scatter_dimension=0, tiled=True)  158 us
    dot_general x1, matrix products, local_step(): lax.dot_general(d_out, w_down, (((1,), (1,)), ((), ())), preferred_elemen...  60.1 us
    dot_general x1, matrix products, local_step(): jnp.einsum('bd,tdc->tbc', trunk_out.astype(jnp.bfloat16), heads, preferre...  46.8 us
    psum x1, blocking collectives, local_step(): full_gram = lax.psum(part_gram, 'data')  42 us
    dot_general x1, matrix products, local_step(): lax.dot_general(hidden, d_out, (((0,), (0,)), ((), ())), preferred_elemen...  39 us
    dot_general x1, matrix products, local_step(): jnp.dot(tok_rows, w_up, preferred_element_type=jnp.float32)  33.9 us
    dot_general x1, matrix products, local_step(): lax.dot_general(tok_rows, d_pre, (((0,), (0,)), ((), ())), preferred_elem...  33.2 us
  transfers between devices with their start and end apart: 2, of which 2 were waited for; matrix products, arithmetic and copies ran while one was open for 15% of the time, Pallas kernels for 0%

commit v1 on v0

v1 whole, which is shorter than its diff:
```python
import functools
import math

import jax
import jax.numpy as jnp
from jax import lax
from jax.experimental import pallas as pl
from jax.experimental.pallas import tpu as pltpu
from jax.sharding import PartitionSpec as P

F32 = jnp.float32
BF16 = jnp.bfloat16
MESH = pl.DeviceIdType.MESH
SOLVER_STEPS = 20
NUM_TASKS = 8
NUM_DEV = 32
NUM_CHIPS = 16
TOK = 2048
PAIR_TOK = 4096
DIM = 1280
HID = 5120
HALF = 2560
TB = 512
NTB = PAIR_TOK // TB
CW = 256
NBLK = HALF // CW
ROWS = 80
C0 = math.sqrt(2.0 / math.pi)
C1 = C0 * 0.044715


def split3(v):
    hi = v.astype(BF16)
    rem = v - hi.astype(F32)
    mid = rem.astype(BF16)
    lo = (rem - mid.astype(F32)).astype(BF16)
    return hi, mid, lo


def dot(a, b, dims=((1,), (0,))):
    return lax.dot_general(a, b, (dims, ((), ())), preferred_element_type=F32)


def remote(src, dst, ssem, rsem, dev):
    return pltpu.make_async_remote_copy(
        src_ref=src, dst_ref=dst, send_sem=ssem, recv_sem=rsem,
        device_id=(dev,), device_id_type=MESH)


def sublane_sum(v):
    for sh in (4, 2, 1):
        v = v + pltpu.roll(v, sh, 0)
    return v


def rolled(v, k):
    return v if k == 0 else pltpu.roll(v, NUM_TASKS - k, 0)


def kernel(x_hbm, w1_hbm, w2_hbm, hc_ref, lab_ref,
           mix_ref, up_hbm, down_ref, a_hbm, xs_hbm,
           wbuf, w1, xt, abuf, gs, gt, agt, dpc, st, st_in, lab_in, rs, r3, tref, tp, trecv, mrecv,
           gbuf, q1, q2, q3, fin,
           wsem, w1sem, xsem, asem, ainsem, pair_s, pair_r, msend, mrec, tsend, trec,
           s1, v1, s2, v2, s3, v3, fs_loc, fs, fv):
    me = lax.axis_index("data")
    core = lax.rem(me, 2)
    chip = me // 2
    cx = lax.rem(chip, 2)
    cy = lax.rem(chip // 2, 2)
    cz = chip // 4
    sib = me + 1 - 2 * core

    def w2_load(c):
        return pltpu.make_async_copy(w2_hbm.at[pl.ds(pl.multiple_of(core * HALF + c * TB, TB), TB)], wbuf.at[c], wsem.at[c])

    def w1_load(c):
        return pltpu.make_async_copy(
            w1_hbm.at[:, pl.ds(pl.multiple_of(core * HALF + c * TB, TB), TB)], w1.at[:, pl.ds(c * TB, TB)], w1sem.at[c])

    def x_load_own(i, slot):
        return pltpu.make_async_copy(x_hbm.at[pl.ds(pl.multiple_of(i * TB, TB), TB)], wbuf.at[slot], xsem.at[slot])

    def x_load_sib(i, slot):
        return pltpu.make_async_copy(xs_hbm.at[pl.ds(pl.multiple_of((i - 4) * TB, TB), TB)], wbuf.at[slot], xsem.at[slot])

    for c in range(5):
        w2_load(c).start()
    for c in range(5):
        w1_load(c).start()

    barrier = pltpu.get_barrier_semaphore()
    for m in range(1, NUM_DEV):
        pl.semaphore_signal(barrier, inc=1, device_id=(lax.rem(me + m, NUM_DEV),), device_id_type=MESH)

    hc = hc_ref[...]
    diff = hc[:NUM_TASKS].astype(F32) - hc[NUM_TASKS:].astype(F32)
    dpieces = jnp.concatenate([p.astype(F32) for p in split3(diff)] + [jnp.zeros((104, DIM), F32)], axis=0)
    dpc[...] = dpieces.T.astype(BF16)
    for c in range(5):
        w2_load(c).wait()
        g24 = dot(wbuf[c], dpc[...])
        if c < 4:
            x_load_own(c, c).start()
        g24t = g24.T
        g8 = g24t[0:8] + g24t[8:16] + g24t[16:24]
        gt[:, c * TB:(c + 1) * TB] = g8
        pieces = jnp.concatenate([p.astype(F32) for p in split3(g8)] + [jnp.zeros((104, TB), F32)], axis=0)
        gs[c * TB:(c + 1) * TB, :] = pieces.T.astype(BF16)

    pl.semaphore_wait(barrier, NUM_DEV - 1)
    x_pair = remote(x_hbm, xs_hbm, pair_s.at[0], pair_r.at[0], sib)
    x_pair.start()
    lab_pair = remote(lab_ref, lab_in, pair_s.at[1], pair_r.at[1], sib)
    lab_pair.start()
    for c in range(5):
        w1_load(c).wait()

    def a_store(par, nb, at):
        return pltpu.make_async_copy(abuf.at[par * NBLK + nb], a_hbm.at[nb, at], asem.at[par, nb])

    def fwd(i, carry):
        slot = lax.rem(i, 5)
        par = lax.rem(i, 2)
        at = lax.rem(core * 4 + i, 8)
        col = pl.multiple_of(at * TB, TB)

        @pl.when(i == 3)
        def _():
            x_pair.wait_recv()

        @pl.when((i >= 3) & (i < 7))
        def _():
            x_load_sib(i + 1, lax.rem(i + 1, 5)).start()

        x_load_own(0, slot).wait()

        @pl.when(i >= 2)
        def _():
            for nb in range(NBLK):
                a_store(par, nb, at).wait()

        xb = wbuf[slot]
        total = None
        for t in range(5):
            pre = dot(xb, w1[:, t * TB:(t + 1) * TB]).astype(BF16)
            abuf[par * NBLK + 2 * t] = pre[:, :CW]
            abuf[par * NBLK + 2 * t + 1] = pre[:, CW:]
            af = pre.astype(F32)
            th = jnp.tanh(af * (C0 + C1 * (af * af)))
            h = 0.5 * af
            pb = (h + h * th).astype(BF16)
            part = dot(pb, gs[t * TB:(t + 1) * TB, :])
            total = part if total is None else total + part
        for nb in range(NBLK):
            a_store(par, nb, at).start()
        xbt = xb.T
        for c in range(NUM_CHIPS):
            zz, yy, xx = c // 4, (c // 2) % 2, c % 2
            xt[xx, yy, zz * ROWS:(zz + 1) * ROWS, pl.ds(col, TB)] = xbt[c * ROWS:(c + 1) * ROWS]
        tt = total.T
        st[:, pl.ds(col, TB)] = tt[0:8] + tt[8:16] + tt[16:24]

        @pl.when(i < 4)
        def _():
            xd = dot(wbuf[slot], dpc[...]).T
            st[:, pl.ds(col, TB)] += xd[0:8] + xd[8:16] + xd[16:24]

        return carry

    lax.fori_loop(0, NTB, fwd, 0)
    for par in range(2):
        for nb in range(NBLK):
            a_store(par, nb, 0).wait()

    st_pair = remote(st, st_in, pair_s.at[2], pair_r.at[2], sib)
    st_pair.start()

    def a_load(j):
        return pltpu.make_async_copy(
            a_hbm.at[j], abuf.at[pl.ds(pl.multiple_of(lax.rem(j, 2) * 8, 8), 8)], ainsem.at[lax.rem(j, 2)])

    a_load(0).start()
    lane = lax.broadcasted_iota(jnp.int32, (NUM_TASKS, 128), 1)
    dgram = jnp.zeros((NUM_TASKS, 128), F32)
    for k in range(NUM_TASKS):
        dgram = jnp.where(lane == k, jnp.sum(diff * rolled(diff, k), axis=1, keepdims=True), dgram)
    lab_pair.wait_recv()
    st_pair.wait_recv()
    own_col = pl.multiple_of(core * TOK, TOK)
    sib_col = pl.multiple_of((1 - core) * TOK, TOK)

    def resid(col, labels):
        delta = st[:, pl.ds(col, TOK)] + st_in[:, pl.ds(col, TOK)]
        sign = jnp.where(labels == 0, -1.0, 1.0)
        u = sign * delta
        e = jnp.exp(-jnp.abs(u))
        return sign * (jnp.where(u >= 0, 1.0, e) / (1.0 + e)) * (1.0 / (TOK * NUM_DEV))

    ra = resid(own_col, lab_ref[...])
    rb = resid(sib_col, lab_in[...])
    first = core == 0
    rlo = jnp.where(first, ra, rb)
    rhi = jnp.where(first, rb, ra)
    cg = jnp.zeros((NUM_TASKS, 128), F32)
    for k in range(NUM_TASKS):
        prod = rlo * rolled(rlo, k) + rhi * rolled(rhi, k)
        cg = jnp.where(lane == k, jnp.sum(prod, axis=1, keepdims=True), cg)
    mrecv[chip] = cg

    def m_copy(m):
        dst = lax.rem(chip + m, NUM_CHIPS) * 2 + core
        return remote(mrecv.at[chip], mrecv.at[chip], msend.at[m - 1], mrec.at[m - 1], dst)

    for m in range(1, NUM_CHIPS):
        m_copy(m).start()

    for part, r in ((0, rlo), (1, rhi)):
        hi, mid, lo = split3(r)
        base = part * TOK
        r3[:, base:base + TOK] = jnp.concatenate([hi.astype(F32), mid.astype(F32), lo.astype(F32), jnp.zeros_like(r)], axis=0).astype(BF16)
        hf, mf, lf = hi.astype(F32), mid.astype(F32), lo.astype(F32)
        for c in range(TOK // TB):
            sl = slice(c * TB, (c + 1) * TB)
            stack = jnp.concatenate([hf[:, sl], hf[:, sl], mf[:, sl], hf[:, sl], lf[:, sl], mf[:, sl], jnp.zeros((80, TB), F32)], axis=0)
            rs[base + c * TB:base + (c + 1) * TB, :] = stack.T.astype(BF16)

    for m in range(1, NUM_CHIPS):
        m_copy(m).wait_recv()
    mp = mrecv[0]
    for c in range(1, NUM_CHIPS):
        mp = mp + mrecv[c]
    mp = mp * dgram
    cols = [jnp.broadcast_to(mp[:, k:k + 1], (NUM_TASKS, 128)) for k in range(NUM_TASKS)]
    inv_scale = NUM_TASKS / sublane_sum(cols[0])

    def solve(step, w):
        ws = [rolled(w, k) for k in range(NUM_TASKS)]
        prods = [cols[k] * ws[k] for k in range(NUM_TASKS)]
        while len(ws) > 1:
            ws = [ws[i] + ws[i + 1] for i in range(0, len(ws), 2)]
            prods = [prods[i] + prods[i + 1] for i in range(0, len(prods), 2)]
        inv = 1.0 / ws[0]
        return (w * inv) * jnp.exp(-(prods[0] * inv) * inv_scale)

    wts = lax.fori_loop(0, SOLVER_STEPS, solve, jnp.full((NUM_TASKS, 128), 1.0 / NUM_TASKS, F32))
    wts = wts / sublane_sum(wts)
    mix_ref[...] = wts
    wcol = wts[:, 0:1]
    hi, mid, lo = [p.astype(F32) for p in split3(gt[...] * wcol)]
    agt[...] = jnp.concatenate([hi, mid, hi, lo, hi, mid, jnp.zeros((80, HALF), F32)], axis=0).astype(BF16)

    def order(j):
        odd = lax.rem(j, 2)
        p1 = (1 - odd) * cx + odd * cy
        p2 = (1 - odd) * cy + odd * cx
        dx = me + 2 * (1 - 2 * cx)
        dy = me + 4 * (1 - 2 * cy)
        return odd, p1, p2, (1 - odd) * dx + odd * dy, (1 - odd) * dy + odd * dx

    def copy1(j):
        odd, p1, p2, d1, d2 = order(j)
        return remote(gbuf.at[j, 1 - p1], q1.at[j], s1.at[j], v1.at[j], d1)

    def copy2(j):
        odd, p1, p2, d1, d2 = order(j)
        return remote(gbuf.at[j, p1, 1 - p2], q2.at[j], s2.at[j], v2.at[j], d2)

    def copy3(j, m):
        odd, p1, p2, d1, d2 = order(j)
        z2 = lax.rem(cz + m, 4)
        dst = z2 * 8 + cy * 4 + cx * 2 + core
        return remote(gbuf.at[j, p1, p2, z2], q3.at[j, m - 1], s3.at[j, m - 1], v3.at[j, m - 1], dst)

    def out_cols(j):
        return pl.ds(pl.multiple_of(core * HALF + j * CW, CW), CW)

    def out_local(j):
        return pltpu.make_async_copy(fin.at[j, core], up_hbm.at[:, out_cols(j)], fs_loc.at[j])

    def out_pair(j):
        return remote(fin.at[j, 1 - core], up_hbm.at[:, out_cols(j)], fs.at[j], fv.at[j], sib)

    def stage2(j):
        odd, p1, p2, d1, d2 = order(j)
        copy1(j).wait_recv()
        gbuf[j, p1, 1 - p2] += q1[j, 1 - p2]
        copy2(j).start()
        gbuf[j, p1, p2] += q1[j, p2]

    def stage3(j):
        odd, p1, p2, d1, d2 = order(j)
        copy2(j).wait_recv()
        gbuf[j, p1, p2] += q2[j]
        for m in (2, 1, 3):
            copy3(j, m).start()

    def finish(j):
        odd, p1, p2, d1, d2 = order(j)
        for m in (1, 2, 3):
            copy3(j, m).wait_recv()
        tot = gbuf[j, p1, p2, cz] + q3[j, 0] + q3[j, 1] + q3[j, 2]
        fin[j, 0] = tot[:ROWS // 2]
        fin[j, 1] = tot[ROWS // 2:]
        out_local(j).start()
        out_pair(j).start()

    def block(j, carry):
        odd, p1, p2, d1, d2 = order(j)
        a_load(j).wait()

        @pl.when(j < NBLK - 1)
        def _():
            a_load(j + 1).start()

        jcol = pl.multiple_of(j * CW, CW)
        base = lax.rem(j, 2) * 8

        def elem(tb, tacc):
            row = pl.multiple_of(tb * TB, TB)
            af = abuf[base + tb].astype(F32)
            dp = dot(rs[pl.ds(row, TB), :], agt[:, pl.ds(jcol, CW)])
            a2 = af * af
            th = jnp.tanh(af * (C0 + C1 * a2))
            h = 0.5 * af
            pb = (h + h * th).astype(BF16)
            slope = (0.5 + 0.5 * th) + (h * (1.0 - th * th)) * (C0 + (3.0 * C1) * a2)
            abuf[16 + tb] = (dp * slope).astype(BF16)
            return tacc + dot(r3[:, pl.ds(row, TB)], pb)

        tacc = lax.fori_loop(0, NTB, elem, jnp.zeros((32, CW), F32))
        tref[:, pl.ds(jcol, CW)] = tacc[0:8] + tacc[8:16] + tacc[16:24]

        def chunk(q, c2):
            a1 = q // 2
            b1 = lax.rem(q, 2)
            i1 = (1 - a1) * (1 - p1) + a1 * p1
            xi = (1 - odd) * i1 + odd * b1
            yi = (1 - odd) * b1 + odd * i1
            g = dot(xt[xi, yi], abuf[16:24].reshape(PAIR_TOK, CW))
            gbuf[j, i1, b1] = g.reshape(4, ROWS, CW)

            @pl.when(q == 1)
            def _():
                copy1(j).start()

            return c2

        lax.fori_loop(0, 4, chunk, 0)

        @pl.when(j >= 1)
        def _():
            stage2(j - 1)

        @pl.when(j >= 2)
        def _():
            stage3(j - 2)

        @pl.when(j >= 3)
        def _():
            finish(j - 3)

        return carry

    lax.fori_loop(0, NBLK, block, 0)

    for i in range(NUM_CHIPS):
        tp[i, :, 0:160] = tref[:, i * 160:(i + 1) * 160]

    def t_copy(i, src_chip):
        return remote(tp.at[i], trecv.at[src_chip], tsend.at[i], trec.at[src_chip], core * 16 + i)

    for i in range(NUM_CHIPS):
        @pl.when(core * 16 + i != me)
        def _():
            t_copy(i, chip).start()

        @pl.when(core * 16 + i == me)
        def _():
            trecv[chip] = tp[i]

    stage2(NBLK - 1)
    stage3(NBLK - 2)
    finish(NBLK - 3)

    for c in range(NUM_CHIPS):
        @pl.when(c * 2 + me // 16 != me)
        def _():
            t_copy(0, c).wait_recv()

    tsum = trecv[0]
    for c in range(1, NUM_CHIPS):
        tsum = tsum + trecv[c]
    down = lax.dot_general(tsum, diff * wcol, (((0,), (0,)), ((), ())), precision=lax.Precision.HIGHEST,
                           preferred_element_type=F32)
    down_ref[...] = down[:160]

    stage3(NBLK - 1)
    finish(NBLK - 2)
    finish(NBLK - 1)

    x_pair.wait_send()
    lab_pair.wait_send()
    st_pair.wait_send()
    for m in range(1, NUM_CHIPS):
        m_copy(m).wait_send()
    for i in range(NUM_CHIPS):
        @pl.when(core * 16 + i != me)
        def _():
            t_copy(i, chip).wait_send()

    def drain(j, carry):
        copy1(j).wait_send()
        copy2(j).wait_send()
        for m in (1, 2, 3):
            copy3(j, m).wait_send()
        out_local(j).wait()
        out_pair(j).wait()
        return carry

    lax.fori_loop(0, NBLK, drain, 0)


def solution(mesh):
    def local_step(tok_rows, w_up, w_down, heads, label_rows):
        hc = jnp.transpose(heads, (2, 0, 1)).reshape(2 * NUM_TASKS, DIM)
        vmem = pl.BlockSpec(memory_space=pltpu.VMEM)
        hbm = pl.BlockSpec(memory_space=pl.ANY)
        sds = jax.ShapeDtypeStruct
        dma = pltpu.SemaphoreType.DMA
        outs = pl.pallas_call(
            kernel,
            out_shape=(
                sds((NUM_TASKS, 128), F32),
                sds((40, HID), F32),
                sds((160, DIM), F32),
                sds((NBLK, NTB, TB, CW), BF16),
                sds((TOK, DIM), BF16),
            ),
            in_specs=[hbm, hbm, hbm, vmem, vmem],
            out_specs=(vmem, hbm, vmem, hbm, hbm),
            scratch_shapes=[
                pltpu.VMEM((5, TB, DIM), BF16),
                pltpu.VMEM((DIM, HALF), BF16),
                pltpu.VMEM((2, 2, 4 * ROWS, PAIR_TOK), BF16),
                pltpu.VMEM((24, TB, CW), BF16),
                pltpu.VMEM((HALF, 128), BF16),
                pltpu.VMEM((NUM_TASKS, HALF), F32),
                pltpu.VMEM((128, HALF), BF16),
                pltpu.VMEM((DIM, 128), BF16),
                pltpu.VMEM((NUM_TASKS, PAIR_TOK), F32),
                pltpu.VMEM((NUM_TASKS, PAIR_TOK), F32),
                pltpu.VMEM((NUM_TASKS, TOK), jnp.int32),
                pltpu.VMEM((PAIR_TOK, 128), BF16),
                pltpu.VMEM((32, PAIR_TOK), BF16),
                pltpu.VMEM((NUM_TASKS, HALF), F32),
                pltpu.VMEM((NUM_CHIPS, NUM_TASKS, 256), F32),
                pltpu.VMEM((NUM_CHIPS, NUM_TASKS, 256), F32),
                pltpu.VMEM((NUM_CHIPS, NUM_TASKS, 128), F32),
                pltpu.VMEM((NBLK, 2, 2, 4, ROWS, CW), F32),
                pltpu.VMEM((NBLK, 2, 4, ROWS, CW), F32),
                pltpu.VMEM((NBLK, 4, ROWS, CW), F32),
                pltpu.VMEM((NBLK, 3, ROWS, CW), F32),
                pltpu.VMEM((NBLK, 2, ROWS // 2, CW), F32),
                dma((5,)), dma((5,)), dma((5,)), dma((2, NBLK)), dma((2,)),
                dma((3,)), dma((3,)), dma((15,)), dma((15,)), dma((16,)), dma((16,)),
                dma((NBLK,)), dma((NBLK,)), dma((NBLK,)), dma((NBLK,)), dma((NBLK, 3)), dma((NBLK, 3)),
                dma((NBLK,)), dma((NBLK,)), dma((NBLK,)),
            ],
            compiler_params=pltpu.CompilerParams(
                collective_id=0, has_side_effects=True, vmem_limit_bytes=67043328),
        )(tok_rows, w_up, w_down, hc, label_rows)
        return outs[0][:, 0], outs[1], outs[2]

    return jax.shard_map(
        local_step, mesh=mesh, in_specs=(P('data', None), P(), P(), P(), P(None, 'data')),
        out_specs=(P(), P('data', None), P('data', None)), check_vma=False)
```

time: 791 us -> 227 us (0.29); the launches traced: 781 us -> 227 us
  waiting for transfers between devices: 446 us -> 0 us
  matrix products: 219 us -> 0 us
  Pallas kernels: 0 us -> 219 us
  blocking collectives: 42 us -> 0 us
  other arithmetic: 28.4 us -> 0 us
  local copies, waits for them, and re-layouts: 29.7 us -> 6.89 us
  between operations: 15 us -> 0.64 us
    unnamed x3 -> x0, waiting for transfers between devices: 288 us -> none
    pallas_call x0 -> x1, Pallas kernels: none -> 219 us  [local_step(): pl.pallas_call(kernel, out_shape=(sds((NUM_TASKS, 128), F32), sds((40, HI...]
    dot_general x8 -> x0, matrix products: 219 us -> none  [the longest x1 60.1 us: local_step(): lax.dot_general(d_out, w_down, (((1,), (1,)), ((), ())), preferred_elemen...]
    reduce_scatter x1 -> x0, waiting for transfers between devices: 158 us -> none  [local_step(): lax.psum_scatter(grad_down, 'data', scatter_dimension=0, tiled=True)]
    psum x1 -> x0, blocking collectives: 42 us -> none  [local_step(): full_gram = lax.psum(part_gram, 'data')]
    unnamed x13 -> x2, local copies, waits for them, and re-layouts: 29.7 us -> 4.17 us
    reduce_sum x42 -> x0, other arithmetic: 15.3 us -> none  [the longest x20 12.4 us: update(): return mix_wts / jnp.sum(mix_wts)]
    div x20 -> x0, other arithmetic: 13 us -> none  [update(): return mix_wts / jnp.sum(mix_wts)]
  transfers between devices with their start and end apart: 2 -> 0, of which waited for: 2 -> 0; matrix products, arithmetic and copies ran while one was open for 15% -> 0% of each run, Pallas kernels for 0% -> 0%
where the time goes in v1:
time: 227 us
  Pallas kernels  219 us (96%)
  local copies, waits for them, and re-layouts  6.89 us (3%)
    pallas_call x1, Pallas kernels, local_step(): pl.pallas_call(kernel, out_shape=(sds((NUM_TASKS, 128), F32), sds((40, HI...  219 us

profile of v1, /device:TPU:0, one launch (start us, length us, event | category | flops | bytes accessed | tf_op | source)
XLA Modules:
  0.0 226.6 jit_solution(15439563892787935259)
XLA Ops:
  0.6 1.4 copy.11
  2.0 219.1 %shard_map.76 = (f32[8,128]{1,0:T(8,128)}, f32[40,5120]{1,0:T(8,128)}, f32[160,1280]{1,0:T(8,128)}, bf16[10,8,512,256]{3,2,1,0:T(8,128)(2,1)}, bf16[2048,1280]{1,0:T(8,128)(2,1)}) custom-call(bf16[2048,1280]{1,0:T(8,128)(2,1)} %x_hbm.1, bf16[1280,5120]{1,0:T(8,128)(2,1)} %w1_hbm.1, bf16[5120,1280]{1,0:T(8,128)(2,1)} %w2_hbm.1, bf16[16,1280]{1,0:T(8,128)(2,1)} %bitcast.4, ...), custom_call_target="tpu_custom_call" | custom-call | tf_op jit(solution)/shard_map/pallas_call | solution.py:431
  221.1 1.3 slice_reduce_fusion
  222.4 2.1 copy.14
  224.5 2.1 copy.15

commit v2 on v1

--- a/solution.py
+++ b/solution.py
@@ -24,6 +24,9 @@
 NTB = PAIR_TOK // TB
 CW = 256
 NBLK = HALF // CW
+UW = 128
+NUNIT = HALF // UW
+LAGS = (1, 3, 4, 6)
 ROWS = 80
 C0 = math.sqrt(2.0 / math.pi)
 C1 = C0 * 0.044715
@@ -60,9 +63,9 @@
 def kernel(x_hbm, w1_hbm, w2_hbm, hc_ref, lab_ref,
            mix_ref, up_hbm, down_ref, a_hbm, xs_hbm,
            wbuf, w1, xt, abuf, gs, gt, agt, dpc, st, st_in, lab_in, rs, r3, tref, tp, trecv, mrecv,
-           gbuf, q1, q2, q3, fin,
+           gbuf, q1, q2, q3, q4, fin,
            wsem, w1sem, xsem, asem, ainsem, pair_s, pair_r, msend, mrec, tsend, trec,
-           s1, v1, s2, v2, s3, v3, fs_loc, fs, fv):
+           rsend, rrecv, fs_loc, fs, fv):
     me = lax.axis_index("data")
     core = lax.rem(me, 2)
     chip = me // 2
@@ -157,7 +160,8 @@
         xbt = xb.T
         for c in range(NUM_CHIPS):
             zz, yy, xx = c // 4, (c // 2) % 2, c % 2
-            xt[xx, yy, zz * ROWS:(zz + 1) * ROWS, pl.ds(col, TB)] = xbt[c * ROWS:(c + 1) * ROWS]
+            row = (yy * 2 + zz // 2) * ROWS
+            xt[zz % 2, xx, row:row + ROWS, pl.ds(col, TB)] = xbt[c * ROWS:(c + 1) * ROWS]
         tt = total.T
         st[:, pl.ds(col, TB)] = tt[0:8] + tt[8:16] + tt[16:24]
 
@@ -250,63 +254,62 @@
     hi, mid, lo = [p.astype(F32) for p in split3(gt[...] * wcol)]
     agt[...] = jnp.concatenate([hi, mid, hi, lo, hi, mid, jnp.zeros((80, HALF), F32)], axis=0).astype(BF16)
 
-    def order(j):
-        odd = lax.rem(j, 2)
-        p1 = (1 - odd) * cx + odd * cy
-        p2 = (1 - odd) * cy + odd * cx
-        dx = me + 2 * (1 - 2 * cx)
-        dy = me + 4 * (1 - 2 * cy)
-        return odd, p1, p2, (1 - odd) * dx + odd * dy, (1 - odd) * dy + odd * dx
-
-    def copy1(j):
-        odd, p1, p2, d1, d2 = order(j)
-        return remote(gbuf.at[j, 1 - p1], q1.at[j], s1.at[j], v1.at[j], d1)
-
-    def copy2(j):
-        odd, p1, p2, d1, d2 = order(j)
-        return remote(gbuf.at[j, p1, 1 - p2], q2.at[j], s2.at[j], v2.at[j], d2)
-
-    def copy3(j, m):
-        odd, p1, p2, d1, d2 = order(j)
-        z2 = lax.rem(cz + m, 4)
-        dst = z2 * 8 + cy * 4 + cx * 2 + core
-        return remote(gbuf.at[j, p1, p2, z2], q3.at[j, m - 1], s3.at[j, m - 1], v3.at[j, m - 1], dst)
-
-    def out_cols(j):
-        return pl.ds(pl.multiple_of(core * HALF + j * CW, CW), CW)
-
-    def out_local(j):
-        return pltpu.make_async_copy(fin.at[j, core], up_hbm.at[:, out_cols(j)], fs_loc.at[j])
-
-    def out_pair(j):
-        return remote(fin.at[j, 1 - core], up_hbm.at[:, out_cols(j)], fs.at[j], fv.at[j], sib)
-
-    def stage2(j):
-        odd, p1, p2, d1, d2 = order(j)
-        copy1(j).wait_recv()
-        gbuf[j, p1, 1 - p2] += q1[j, 1 - p2]
-        copy2(j).start()
-        gbuf[j, p1, p2] += q1[j, p2]
-
-    def stage3(j):
-        odd, p1, p2, d1, d2 = order(j)
-        copy2(j).wait_recv()
-        gbuf[j, p1, p2] += q2[j]
-        for m in (2, 1, 3):
-            copy3(j, m).start()
-
-    def finish(j):
-        odd, p1, p2, d1, d2 = order(j)
-        for m in (1, 2, 3):
-            copy3(j, m).wait_recv()
-        tot = gbuf[j, p1, p2, cz] + q3[j, 0] + q3[j, 1] + q3[j, 2]
-        fin[j, 0] = tot[:ROWS // 2]
-        fin[j, 1] = tot[ROWS // 2:]
-        out_local(j).start()
-        out_pair(j).start()
+    zl = lax.rem(cz, 2)
+    zh = cz // 2
+    to_x = me + 2 * (1 - 2 * cx)
+    to_y = me + 4 * (1 - 2 * cy)
+    to_zl = me + 8 * (1 - 2 * zl)
+    to_zh = me + 16 * (1 - 2 * zh)
+    pos1, pos2 = (cx, cy), (cy, cx)
+    dev1, dev3 = (to_x, to_y), (to_y, to_x)
+
+    def copy(j, h, s):
+        u = 2 * j + h
+        p1, p2 = pos1[h], pos2[h]
+        if s == 1:
+            src, dst, dev = gbuf.at[u, 1 - p1], q1.at[u], dev1[h]
+        elif s == 2:
+            src, dst, dev = gbuf.at[u, p1, 1 - zl], q2.at[u], to_zl
+        elif s == 3:
+            src, dst, dev = gbuf.at[u, p1, zl, 1 - p2], q3.at[u], dev3[h]
+        else:
+            src, dst, dev = gbuf.at[u, p1, zl, p2, 1 - zh], q4.at[u], to_zh
+        return remote(src, dst, rsend.at[s - 1, u], rrecv.at[s - 1, u], dev)
+
+    def out_cols(u):
+        return pl.ds(pl.multiple_of(core * HALF + u * UW, UW), UW)
+
+    def out_local(u):
+        return pltpu.make_async_copy(fin.at[u, core], up_hbm.at[:, out_cols(u)], fs_loc.at[u])
+
+    def out_pair(u):
+        return remote(fin.at[u, 1 - core], up_hbm.at[:, out_cols(u)], fs.at[u], fv.at[u], sib)
+
+    def stage(j, s):
+        for h in range(2):
+            u = 2 * j + h
+            p1, p2 = pos1[h], pos2[h]
+            copy(j, h, s - 1).wait_recv()
+            if s == 2:
+                gbuf[u, p1, 1 - zl] += q1[u, 1 - zl]
+                copy(j, h, 2).start()
+                gbuf[u, p1, zl] += q1[u, zl]
+            elif s == 3:
+                gbuf[u, p1, zl, 1 - p2] += q2[u, 1 - p2]
+                copy(j, h, 3).start()
+                gbuf[u, p1, zl, p2] += q2[u, p2]
+            elif s == 4:
+                gbuf[u, p1, zl, p2, 1 - zh] += q3[u, 1 - zh]
+                copy(j, h, 4).start()
+                gbuf[u, p1, zl, p2, zh] += q3[u, zh]
+            else:
+                tot = gbuf[u, p1, zl, p2, zh] + q4[u]
+                fin[u, 0] = tot[:ROWS // 2]
+                fin[u, 1] = tot[ROWS // 2:]
+                out_local(u).start()
+                out_pair(u).start()
 
     def block(j, carry):
-        odd, p1, p2, d1, d2 = order(j)
         a_load(j).wait()
 
         @pl.when(j < NBLK - 1)
@@ -332,33 +335,26 @@
         tref[:, pl.ds(jcol, CW)] = tacc[0:8] + tacc[8:16] + tacc[16:24]
 
         def chunk(q, c2):
-            a1 = q // 2
-            b1 = lax.rem(q, 2)
-            i1 = (1 - a1) * (1 - p1) + a1 * p1
-            xi = (1 - odd) * i1 + odd * b1
-            yi = (1 - odd) * b1 + odd * i1
-            g = dot(xt[xi, yi], abuf[16:24].reshape(PAIR_TOK, CW))
-            gbuf[j, i1, b1] = g.reshape(4, ROWS, CW)
+            far = 1 - q // 2
+            xi = far * (1 - cx) + (1 - far) * cx
+            zi = lax.rem(q, 2)
+            g = dot(xt[zi, xi], abuf[16:24].reshape(PAIR_TOK, CW)).reshape(2, 2, ROWS, CW)
+            gbuf[2 * j, xi, zi] = g[:, :, :, :UW]
+            for yi in range(2):
+                gbuf[2 * j + 1, yi, zi, xi] = g[yi, :, :, UW:]
 
             @pl.when(q == 1)
             def _():
-                copy1(j).start()
+                copy(j, 0, 1).start()
 
             return c2
 
         lax.fori_loop(0, 4, chunk, 0)
-
-        @pl.when(j >= 1)
-        def _():
-            stage2(j - 1)
-
-        @pl.when(j >= 2)
-        def _():
-            stage3(j - 2)
-
-        @pl.when(j >= 3)
-        def _():
-            finish(j - 3)
+        copy(j, 1, 1).start()
+        for s, lag in zip((2, 3, 4, 5), LAGS):
+            @pl.when(j >= lag)
+            def _():
+                stage(j - lag, s)
 
         return carry
 
@@ -379,9 +375,13 @@
         def _():
             trecv[chip] = tp[i]
 
-    stage2(NBLK - 1)
-    stage3(NBLK - 2)
-    finish(NBLK - 3)
+    def late(b):
+        for s, lag in zip((2, 3, 4, 5), LAGS):
+            if b - lag < NBLK:
+                stage(b - lag, s)
+
+    late(NBLK)
+    late(NBLK + 1)
 
     for c in range(NUM_CHIPS):
         @pl.when(c * 2 + me // 16 != me)
@@ -395,9 +395,8 @@
                            preferred_element_type=F32)
     down_ref[...] = down[:160]
 
-    stage3(NBLK - 1)
-    finish(NBLK - 2)
-    finish(NBLK - 1)
+    for b in range(NBLK + 2, NBLK + LAGS[3]):
+        late(b)
 
     x_pair.wait_send()
     lab_pair.wait_send()
@@ -410,15 +409,37 @@
             t_copy(i, chip).wait_send()
 
     def drain(j, carry):
-        copy1(j).wait_send()
-        copy2(j).wait_send()
-        for m in (1, 2, 3):
-            copy3(j, m).wait_send()
-        out_local(j).wait()
-        out_pair(j).wait()
+        for h in range(2):
+            for s in range(1, 5):
+                copy(j, h, s).wait_send()
+            out_local(2 * j + h).wait()
+            out_pair(2 * j + h).wait()
         return carry
 
     lax.fori_loop(0, NBLK, drain, 0)
+
+
+def place(mix_in, up_in, down_in, mix_ref, up_hbm, down_hbm, ubuf, dbuf, sem):
+    loads, stores = [], []
+    for c in range(4):
+        cu, cd = pl.ds(c * 1280, 1280), pl.ds(c * 40, 40)
+        loads.append((pltpu.make_async_copy(up_in.at[:, cu], ubuf.at[:, cu], sem.at[0, c]),
+                      pltpu.make_async_copy(down_in.at[cd], dbuf.at[cd], sem.at[1, c])))
+        stores.append((pltpu.make_async_copy(ubuf.at[:, cu], up_hbm.at[:, cu], sem.at[2, c]),
+                       pltpu.make_async_copy(dbuf.at[cd], down_hbm.at[cd], sem.at[3, c])))
+    for pair in loads:
+        for cp in pair:
+            cp.start()
+    w = mix_in[...]
+    diag = lax.broadcasted_iota(jnp.int32, w.shape, 0) == lax.broadcasted_iota(jnp.int32, w.shape, 1)
+    mix_ref[...] = jnp.sum(jnp.where(diag, w, 0.0), axis=0)[:NUM_TASKS]
+    for ld, stp in zip(loads, stores):
+        for a, b in zip(ld, stp):
+            a.wait()
+            b.start()
+    for pair in stores:
+        for cp in pair:
+            cp.wait()
 
 
 def solution(mesh):
@@ -457,20 +478,26 @@
                 pltpu.VMEM((NUM_CHIPS, NUM_TASKS, 256), F32),
                 pltpu.VMEM((NUM_CHIPS, NUM_TASKS, 256), F32),
                 pltpu.VMEM((NUM_CHIPS, NUM_TASKS, 128), F32),
-                pltpu.VMEM((NBLK, 2, 2, 4, ROWS, CW), F32),
-                pltpu.VMEM((NBLK, 2, 4, ROWS, CW), F32),
-                pltpu.VMEM((NBLK, 4, ROWS, CW), F32),
-                pltpu.VMEM((NBLK, 3, ROWS, CW), F32),
-                pltpu.VMEM((NBLK, 2, ROWS // 2, CW), F32),
+                pltpu.VMEM((NUNIT, 2, 2, 2, 2, ROWS, UW), F32),
+                pltpu.VMEM((NUNIT, 2, 2, 2, ROWS, UW), F32),
+                pltpu.VMEM((NUNIT, 2, 2, ROWS, UW), F32),
+                pltpu.VMEM((NUNIT, 2, ROWS, UW), F32),
+                pltpu.VMEM((NUNIT, ROWS, UW), F32),
+                pltpu.VMEM((NUNIT, 2, ROWS // 2, UW), F32),
                 dma((5,)), dma((5,)), dma((5,)), dma((2, NBLK)), dma((2,)),
                 dma((3,)), dma((3,)), dma((15,)), dma((15,)), dma((16,)), dma((16,)),
-                dma((NBLK,)), dma((NBLK,)), dma((NBLK,)), dma((NBLK,)), dma((NBLK, 3)), dma((NBLK, 3)),
-                dma((NBLK,)), dma((NBLK,)), dma((NBLK,)),
+                dma((4, NUNIT)), dma((4, NUNIT)), dma((NUNIT,)), dma((NUNIT,)), dma((NUNIT,)),
             ],
             compiler_params=pltpu.CompilerParams(
                 collective_id=0, has_side_effects=True, vmem_limit_bytes=67043328),
         )(tok_rows, w_up, w_down, hc, label_rows)
-        return outs[0][:, 0], outs[1], outs[2]
+        return pl.pallas_call(
+            place,
+            out_shape=(sds((NUM_TASKS,), F32), sds((40, HID), F32), sds((160, DIM), F32)),
+            in_specs=[vmem, hbm, hbm],
+            out_specs=(vmem, hbm, hbm),
+            scratch_shapes=[pltpu.VMEM((40, HID), F32), pltpu.VMEM((160, DIM), F32), dma((4, 4))],
+        )(*outs[:3])
 
     return jax.shard_map(
         local_step, mesh=mesh, in_specs=(P('data', None), P(), P(), P(), P(None, 'data')),

time: 227 us -> 181 us (0.80)
  Pallas kernels: 219 us -> 178 us
  local copies, waits for them, and re-layouts: 6.89 us -> 1.4 us
    pallas_call x1, Pallas kernels: 219 us -> 175 us  [local_step(): pl.pallas_call(kernel, out_shape=(sds((NUM_TASKS, 128), F32), sds((40, HI...]
    unnamed x2 -> x0, local copies, waits for them, and re-layouts: 4.17 us -> none
    pallas_call x0 -> x1, Pallas kernels: none -> 3.5 us  [local_step(): pl.pallas_call(place, out_shape=(sds((NUM_TASKS,), F32), sds((40, HID), F...]
where the time goes in v2:
time: 181 us; the launch traced here: 180 us
  Pallas kernels  178 us (98%)
    pallas_call x1, Pallas kernels, local_step(): pl.pallas_call(kernel, out_shape=(sds((NUM_TASKS, 128), F32), sds((40, HI...  175 us

profile of v2, /device:TPU:0, one launch (start us, length us, event | category | flops | bytes accessed | tf_op | source)
XLA Modules:
  0.0 180.4 jit_solution(1626639063894477861)
XLA Ops:
  0.6 1.4 copy.10
  2.0 174.8 %shard_map.76 = (f32[8,128]{1,0:T(8,128)}, f32[40,5120]{1,0:T(8,128)}, f32[160,1280]{1,0:T(8,128)}, bf16[10,8,512,256]{3,2,1,0:T(8,128)(2,1)}, bf16[2048,1280]{1,0:T(8,128)(2,1)}) custom-call(bf16[2048,1280]{1,0:T(8,128)(2,1)} %x_hbm.1, bf16[1280,5120]{1,0:T(8,128)(2,1)} %w1_hbm.1, bf16[5120,1280]{1,0:T(8,128)(2,1)} %w2_hbm.1, bf16[16,1280]{1,0:T(8,128)(2,1)} %bitcast.4, ...), custom_call_target="tpu_custom_call" | custom-call | tf_op jit(solution)/shard_map/pallas_call | solution.py:452
  176.9 3.5 %shard_map.77 = (f32[8]{0:T(128)}, f32[40,5120]{1,0:T(8,128)}, f32[160,1280]{1,0:T(8,128)}) custom-call(f32[8,128]{1,0:T(8,128)} %get-tuple-element.6.mix_in, f32[40,5120]{1,0:T(8,128)} %get-tuple-element.7.up_in, f32[160,1280]{1,0:T(8,128)} %get-tuple-element.8.down_in), custom_call_target="tpu_custom_call" | custom-call | tf_op jit(solution)/shard_map/pallas_call | solution.py:494

commit v3 on v2

v3 whole, which is shorter than its diff:
```python
import functools
import math

import jax
import jax.numpy as jnp
from jax import lax
from jax.experimental import pallas as pl
from jax.experimental.pallas import tpu as pltpu
from jax.sharding import PartitionSpec as P

F32 = jnp.float32
BF16 = jnp.bfloat16
MESH = pl.DeviceIdType.MESH
SOLVER_STEPS = 20
NUM_TASKS = 8
NUM_DEV = 32
NUM_CHIPS = 16
TOK = 2048
PAIR_TOK = 4096
DIM = 1280
HID = 5120
HALF = 2560
TB = 512
NTB = PAIR_TOK // TB
CW = 256
NBLK = HALF // CW
UW = 128
NUNIT = HALF // UW
PLAN = ((0, 2, 1), (1, 3, 3), (1, 4, 4), (2, 5, 6))
ROWS = 80
C0 = math.sqrt(2.0 / math.pi)
C1 = C0 * 0.044715


def split3(v):
    hi = v.astype(BF16)
    rem = v - hi.astype(F32)
    mid = rem.astype(BF16)
    lo = (rem - mid.astype(F32)).astype(BF16)
    return hi, mid, lo


def dot(a, b, dims=((1,), (0,))):
    return lax.dot_general(a, b, (dims, ((), ())), preferred_element_type=F32)


def remote(src, dst, ssem, rsem, dev):
    return pltpu.make_async_remote_copy(
        src_ref=src, dst_ref=dst, send_sem=ssem, recv_sem=rsem,
        device_id=(dev,), device_id_type=MESH)


def sublane_sum(v):
    for sh in (4, 2, 1):
        v = v + pltpu.roll(v, sh, 0)
    return v


def rolled(v, k):
    return v if k == 0 else pltpu.roll(v, NUM_TASKS - k, 0)


def kernel(x_hbm, w1_hbm, w2_hbm, hc_ref, lab_ref,
           mix_ref, up_hbm, tsum_ref, ad_ref, a_hbm, xs_hbm,
           wbuf, w1, xt, abuf, da0, da1, pref, stx, gs, gt, dpc, st, st_in, lab_in, r3, tref, tp, trecv, mrecv,
           gbuf, q1, q2, q3, q4,
           w2sem, w1sem, xsem, asem, ainsem, pair_s, pair_r, msend, mrec, tsend, trec,
           rsend, rrecv, fs_loc, fs, fv):
    me = lax.axis_index("data")
    core = lax.rem(me, 2)
    chip = me // 2
    cx = lax.rem(chip, 2)
    cy = lax.rem(chip // 2, 2)
    cz = chip // 4
    sib = me + 1 - 2 * core

    def w2_tile(n):
        return da0.at[n] if n < 8 else da1.at[n - 8] if n < 16 else abuf.at[n - 6]

    def w2_load(n):
        rows = pl.ds(pl.multiple_of(core * HALF + n // 5 * TB, TB), TB)
        return pltpu.make_async_copy(w2_hbm.at[rows, pl.ds(n % 5 * CW, CW)], w2_tile(n), w2sem.at[n])

    def w1_load(c):
        return pltpu.make_async_copy(
            w1_hbm.at[:, pl.ds(pl.multiple_of(core * HALF + c * TB, TB), TB)], w1.at[:, pl.ds(c * TB, TB)], w1sem.at[c])

    def x_load_own(i):
        return pltpu.make_async_copy(x_hbm.at[pl.ds(i * TB, TB)], wbuf.at[i], xsem.at[i])

    def x_load_sib(i, slot):
        return pltpu.make_async_copy(xs_hbm.at[pl.ds(pl.multiple_of((i - 4) * TB, TB), TB)], wbuf.at[slot], xsem.at[slot])

    x_load_own(0).start()
    for c in range(5):
        w1_load(c).start()
    for c in range(1, 4):
        x_load_own(c).start()
    for n in range(25):
        w2_load(n).start()

    barrier = pltpu.get_barrier_semaphore()
    for m in range(1, NUM_DEV):
        pl.semaphore_signal(barrier, inc=1, device_id=(lax.rem(me + m, NUM_DEV),), device_id_type=MESH)

    def fold(v):
        return v[0:8] + v[8:16] + v[16:24]

    def wide(parts, rows, cols):
        return jnp.concatenate([p.astype(F32) for p in parts] + [jnp.zeros((128 - rows, cols), F32)], axis=0)

    diff = hc_ref[:, 0, :].astype(F32) - hc_ref[:, 1, :].astype(F32)
    dpc[...] = wide(split3(diff), 24, DIM).T.astype(BF16)
    def a_store(par, nb, at):
        return pltpu.make_async_copy(abuf.at[par * NBLK + nb], a_hbm.at[nb, at], asem.at[par, nb])

    def gelu16(v):
        af = v.astype(F32)
        h = 0.5 * af
        return (h + h * jnp.tanh(af * (C0 + C1 * (af * af)))).astype(BF16)

    def block_col(i):
        return pl.multiple_of(lax.rem(core * 4 + i, 8) * TB, TB)

    def finish_prev(par, col):
        tot = dot(pref[...], gs[0:4 * TB, :])
        for n in (8, 9):
            tot = tot + dot(gelu16(abuf[par * NBLK + n]), gs[n * CW:(n + 1) * CW, :])
        st[:, pl.ds(col, TB)] = fold(tot.T)

    def fwd_block(i, first):
        slot = lax.rem(i, 4)
        par = lax.rem(i, 2)
        at = lax.rem(core * 4 + i, 8)
        col = block_col(i)

        if first:
            x_load_own(0).wait()
        else:
            @pl.when(i == 3)
            def _():
                x_pair.wait_recv()

            @pl.when((i >= 3) & (i < 7))
            def _():
                x_load_sib(i + 1, lax.rem(i + 1, 4)).start()

            @pl.when(i >= 4)
            def _():
                x_load_sib(i, slot).wait()

            @pl.when(i >= 2)
            def _():
                for nb in range(NBLK):
                    a_store(par, nb, at).wait()

        xb = wbuf[slot]

        def tile(t):
            if first:
                w1_load(t).wait()
            pre = dot(xb, w1[:, t * TB:(t + 1) * TB]).astype(BF16)
            abuf[par * NBLK + 2 * t] = pre[:, :CW]
            abuf[par * NBLK + 2 * t + 1] = pre[:, CW:]
            return pre

        pre = tile(0)
        if not first:
            finish_prev(1 - par, block_col(i + 7))
        pref[:, 0:TB] = gelu16(pre)
        for t in range(1, 4):
            pref[:, t * TB:(t + 1) * TB] = gelu16(tile(t))
        tile(4)
        xbt = xb.T
        for c in range(NUM_CHIPS):
            zz, yy, xx = c // 4, (c // 2) % 2, c % 2
            row = (yy * 2 + zz // 2) * ROWS
            xt[zz % 2, xx, row:row + ROWS, pl.ds(col, TB)] = xbt[c * ROWS:(c + 1) * ROWS]
        for nb in range(NBLK):
            a_store(par, nb, at).start()

    fwd_block(0, True)

    for c in range(1, 4):
        x_load_own(c).wait()
    for n in range(25):
        w2_load(n).wait()
    for c in range(4):
        stx[:, c * TB:(c + 1) * TB] = fold(dot(wbuf[c], dpc[...]).T)
    for c in range(5):
        g24 = dot(w2_tile(5 * c)[...], dpc[0:CW, :])
        for kc in range(1, 5):
            g24 = g24 + dot(w2_tile(5 * c + kc)[...], dpc[kc * CW:(kc + 1) * CW, :])
        g8 = fold(g24.T)
        gt[:, c * TB:(c + 1) * TB] = g8
        gs[c * TB:(c + 1) * TB, :] = wide(split3(g8), 24, TB).T.astype(BF16)

    pl.semaphore_wait(barrier, NUM_DEV - 1)
    x_pair = remote(x_hbm, xs_hbm, pair_s.at[0], pair_r.at[0], sib)
    x_pair.start()
    lab_pair = remote(lab_ref, lab_in, pair_s.at[1], pair_r.at[1], sib)
    lab_pair.start()

    def fwd(i, carry):
        fwd_block(i, False)
        return carry

    lax.fori_loop(1, NTB, fwd, 0)
    finish_prev(1, block_col(7))
    own = pl.ds(pl.multiple_of(core * TOK, TOK), TOK)
    st[:, own] += stx[...]
    for par in range(2):
        for nb in range(NBLK):
            a_store(par, nb, 0).wait()

    st_pair = remote(st, st_in, pair_s.at[2], pair_r.at[2], sib)
    st_pair.start()

    def a_load(j):
        return pltpu.make_async_copy(
            a_hbm.at[j], abuf.at[pl.ds(pl.multiple_of(lax.rem(j, 2) * 8, 8), 8)], ainsem.at[lax.rem(j, 2)])

    a_load(0).start()
    a_load(1).start()
    agt = w1.at[0:128]

    def resid_tile(tb):
        return wbuf.at[lax.rem(tb, 4), :, pl.ds(pl.multiple_of(tb // 4 * 128, 128), 128)]

    lane = lax.broadcasted_iota(jnp.int32, (NUM_TASKS, 128), 1)
    dgram = jnp.zeros((NUM_TASKS, 128), F32)
    for k in range(NUM_TASKS):
        dgram = jnp.where(lane == k, jnp.sum(diff * rolled(diff, k), axis=1, keepdims=True), dgram)
    lab_pair.wait_recv()
    st_pair.wait_recv()
    own_col = pl.multiple_of(core * TOK, TOK)
    sib_col = pl.multiple_of((1 - core) * TOK, TOK)

    def resid(col, labels):
        delta = st[:, pl.ds(col, TOK)] + st_in[:, pl.ds(col, TOK)]
        sign = jnp.where(labels == 0, -1.0, 1.0)
        u = sign * delta
        e = jnp.exp(-jnp.abs(u))
        return sign * (jnp.where(u >= 0, 1.0, e) / (1.0 + e)) * (1.0 / (TOK * NUM_DEV))

    ra = resid(own_col, lab_ref[...])
    rb = resid(sib_col, lab_in[...])
    first = core == 0
    rlo = jnp.where(first, ra, rb)
    rhi = jnp.where(first, rb, ra)
    cg = jnp.zeros((NUM_TASKS, 128), F32)
    for k in range(NUM_TASKS):
        prod = rlo * rolled(rlo, k) + rhi * rolled(rhi, k)
        cg = jnp.where(lane == k, jnp.sum(prod, axis=1, keepdims=True), cg)
    mrecv[chip] = cg

    def m_copy(m):
        dst = lax.rem(chip + m, NUM_CHIPS) * 2 + core
        return remote(mrecv.at[chip], mrecv.at[chip], msend.at[m - 1], mrec.at[m - 1], dst)

    for m in range(1, NUM_CHIPS):
        m_copy(m).start()

    for part, r in ((0, rlo), (1, rhi)):
        hi, mid, lo = split3(r)
        base = part * TOK
        r3[:, base:base + TOK] = jnp.concatenate([hi.astype(F32), mid.astype(F32), lo.astype(F32), jnp.zeros_like(r)], axis=0).astype(BF16)
        hf, mf, lf = hi.astype(F32), mid.astype(F32), lo.astype(F32)
        for c in range(TOK // TB):
            sl = slice(c * TB, (c + 1) * TB)
            stack = jnp.concatenate([hf[:, sl], hf[:, sl], mf[:, sl], hf[:, sl], lf[:, sl], mf[:, sl], jnp.zeros((80, TB), F32)], axis=0)
            wbuf[c, :, part * 128:(part + 1) * 128] = stack.T.astype(BF16)

    def slope_of(af):
        a2 = af * af
        th = jnp.tanh(af * (C0 + C1 * a2))
        h = 0.5 * af
        slope = (0.5 + 0.5 * th) + (h * (1.0 - th * th)) * (C0 + (3.0 * C1) * a2)
        return (h + h * th).astype(BF16), slope

    a_load(0).wait()

    def slope0(tb, tacc):
        pb, slope = slope_of(abuf[tb].astype(F32))
        for h in range(2):
            gbuf[12 + tb, h, :, :, :, 0:64] = slope[:, h * UW:(h + 1) * UW].reshape(2, 2, 2, 64, UW)
        return tacc + dot(r3[:, pl.ds(pl.multiple_of(tb * TB, TB), TB)], pb)

    tacc = lax.fori_loop(0, NTB, slope0, jnp.zeros((32, CW), F32))
    tref[:, 0:CW] = fold(tacc)

    for m in range(1, NUM_CHIPS):
        m_copy(m).wait_recv()
    mp = mrecv[0]
    for c in range(1, NUM_CHIPS):
        mp = mp + mrecv[c]
    mp = mp * dgram
    cols = [jnp.broadcast_to(mp[:, k:k + 1], (NUM_TASKS, 128)) for k in range(NUM_TASKS)]
    inv_scale = NUM_TASKS / sublane_sum(cols[0])

    def solve(step, w):
        ws = [rolled(w, k) for k in range(NUM_TASKS)]
        prods = [cols[k] * ws[k] for k in range(NUM_TASKS)]
        while len(ws) > 1:
            ws = [ws[i] + ws[i + 1] for i in range(0, len(ws), 2)]
            prods = [prods[i] + prods[i + 1] for i in range(0, len(prods), 2)]
        inv = 1.0 / ws[0]
        return (w * inv) * jnp.exp(-(prods[0] * inv) * inv_scale)

    wts = lax.fori_loop(0, SOLVER_STEPS, solve, jnp.full((NUM_TASKS, 128), 1.0 / NUM_TASKS, F32))
    wts = wts / sublane_sum(wts)
    mix_ref[...] = wts
    wcol = wts[:, 0:1]
    hi, mid, lo = [p.astype(F32) for p in split3(gt[...] * wcol)]
    agt[...] = jnp.concatenate([hi, mid, hi, lo, hi, mid, jnp.zeros((80, HALF), F32)], axis=0).astype(BF16)

    zl = lax.rem(cz, 2)
    zh = cz // 2
    to_x = me + 2 * (1 - 2 * cx)
    to_y = me + 4 * (1 - 2 * cy)
    to_zl = me + 8 * (1 - 2 * zl)
    to_zh = me + 16 * (1 - 2 * zh)
    pos1, pos2 = (cx, cy), (cy, cx)
    dev1, dev3 = (to_x, to_y), (to_y, to_x)

    def copy(j, h, s):
        u = 2 * j + h
        p1, p2 = pos1[h], pos2[h]
        if s < 2:
            zi = 1 - zl if s == 0 else zl
            src, dst, dev = gbuf.at[u, 1 - p1, zi], q1.at[u, zi], dev1[h]
        elif s == 2:
            src, dst, dev = gbuf.at[u, p1, 1 - zl], q2.at[u], to_zl
        elif s == 3:
            src, dst, dev = gbuf.at[u, p1, zl, 1 - p2], q3.at[u], dev3[h]
        else:
            src, dst, dev = gbuf.at[u, p1, zl, p2, 1 - zh], q4.at[u], to_zh
        return remote(src, dst, rsend.at[s, u], rrecv.at[s, u], dev)

    def out_cols(u):
        return pl.ds(pl.multiple_of(core * HALF + u * UW, UW), UW)

    def result(u, half):
        h = lax.rem(u, 2)
        p1 = (1 - h) * cx + h * cy
        p2 = (1 - h) * cy + h * cx
        return gbuf.at[u, p1, zl, p2, zh, pl.ds(pl.multiple_of(half * (ROWS // 2), 8), ROWS // 2)]

    def out_local(u):
        return pltpu.make_async_copy(result(u, core), up_hbm.at[:, out_cols(u)], fs_loc.at[u])

    def out_pair(u):
        return remote(result(u, 1 - core), up_hbm.at[:, out_cols(u)], fs.at[u], fv.at[u], sib)

    def stage(j, s):
        for h in range(2):
            u = 2 * j + h
            p1, p2 = pos1[h], pos2[h]
            if s == 2:
                copy(j, h, 0).wait_recv()
                gbuf[u, p1, 1 - zl] += q1[u, 1 - zl]
                copy(j, h, 2).start()
            elif s == 3:
                copy(j, h, 1).wait_recv()
                copy(j, h, 2).wait_recv()
                gbuf[u, p1, zl, 1 - p2] += q1[u, zl, 1 - p2] + q2[u, 1 - p2]
                copy(j, h, 3).start()
                gbuf[u, p1, zl, p2] += q1[u, zl, p2] + q2[u, p2]
            elif s == 4:
                copy(j, h, 3).wait_recv()
                gbuf[u, p1, zl, p2, 1 - zh] += q3[u, 1 - zh]
                copy(j, h, 4).start()
                gbuf[u, p1, zl, p2, zh] += q3[u, zh]
            else:
                copy(j, h, 4).wait_recv()
                gbuf[u, p1, zl, p2, zh] += q4[u]
                out_local(u).start()
                out_pair(u).start()

    def elem0(tb, carry):
        dp = dot(resid_tile(tb)[...], agt[:, 0:CW])
        for h in range(2):
            slope = gbuf[12 + tb, h, :, :, :, 0:64].reshape(TB, UW)
            da0[tb, :, h * UW:(h + 1) * UW] = (dp[:, h * UW:(h + 1) * UW] * slope).astype(BF16)
        return carry

    lax.fori_loop(0, NTB, elem0, 0)

    def block(j, cur, nxt):
        @pl.when(j < NBLK - 1)
        def _():
            a_load(j + 1).wait()

        @pl.when(j < NBLK - 2)
        def _():
            a_load(j + 2).start()

        ncol = pl.multiple_of(jnp.minimum(j + 1, NBLK - 1) * CW, CW)
        base = lax.rem(j + 1, 2) * 8

        def chunk(q, tacc):
            far = 1 - lax.rem(q, 2)
            xi = far * (1 - cx) + (1 - far) * cx
            near = q // 2
            zi = (1 - near) * (1 - zl) + near * zl
            g = dot(xt[zi, xi], cur[...].reshape(PAIR_TOK, CW)).reshape(2, 2, ROWS, CW)
            gbuf[2 * j, xi, zi] = g[:, :, :, :UW]
            for yi in range(2):
                gbuf[2 * j + 1, yi, zi, xi] = g[yi, :, :, UW:]
            for n in range(2):
                tb = 2 * q + n
                rows = pl.ds(pl.multiple_of(tb * TB, TB), TB)
                pb, slope = slope_of(abuf[base + tb].astype(F32))
                dp = dot(resid_tile(tb)[...], agt[:, pl.ds(ncol, CW)])
                nxt[tb] = (dp * slope).astype(BF16)
                tacc = tacc + dot(r3[:, rows], pb)

            for k, (h, part) in enumerate(((0, 0), (1, 0), (0, 1), (1, 1))):
                @pl.when(q == k)
                def _():
                    copy(j, h, part).start()

            for k, s, lag in PLAN:
                @pl.when((q == k) & (j >= lag))
                def _():
                    stage(j - lag, s)

            return tacc

        tacc = lax.fori_loop(0, 4, chunk, jnp.zeros((32, CW), F32))

        @pl.when(j < NBLK - 1)
        def _():
            tref[:, pl.ds(ncol, CW)] = fold(tacc)

    def two_blocks(jj, carry):
        block(2 * jj, da0, da1)
        block(2 * jj + 1, da1, da0)
        return carry

    lax.fori_loop(0, NBLK // 2, two_blocks, 0)

    for i in range(NUM_CHIPS):
        tp[i, :, 0:160] = tref[:, i * 160:(i + 1) * 160]

    def t_copy(i, src_chip):
        return remote(tp.at[i], trecv.at[src_chip], tsend.at[i], trec.at[src_chip], core * 16 + i)

    for i in range(NUM_CHIPS):
        @pl.when(core * 16 + i != me)
        def _():
            t_copy(i, chip).start()

        @pl.when(core * 16 + i == me)
        def _():
            trecv[chip] = tp[i]

    def late(b):
        for _, s, lag in PLAN:
            if b - lag < NBLK:
                stage(b - lag, s)

    late(NBLK)
    late(NBLK + 1)

    for c in range(NUM_CHIPS):
        @pl.when(c * 2 + me // 16 != me)
        def _():
            t_copy(0, c).wait_recv()

    tsum = trecv[0]
    for c in range(1, NUM_CHIPS):
        tsum = tsum + trecv[c]
    tsum_ref[...] = tsum
    ad_ref[...] = diff * wcol

    for b in range(NBLK + 2, NBLK + PLAN[-1][2]):
        late(b)

    x_pair.wait_send()
    lab_pair.wait_send()
    st_pair.wait_send()
    for m in range(1, NUM_CHIPS):
        m_copy(m).wait_send()
    for i in range(NUM_CHIPS):
        @pl.when(core * 16 + i != me)
        def _():
            t_copy(i, chip).wait_send()

    def drain(j, carry):
        for h in range(2):
            for s in range(5):
                copy(j, h, s).wait_send()
            out_local(2 * j + h).wait()
            out_pair(2 * j + h).wait()
        return carry

    lax.fori_loop(0, NBLK, drain, 0)


def place(mix_in, up_in, tsum_in, ad_in, mix_ref, up_hbm, down_hbm, ubuf, dbuf, sem):
    cols = [pl.ds(c * 1280, 1280) for c in range(4)]
    loads = [pltpu.make_async_copy(up_in.at[:, cu], ubuf.at[:, cu], sem.at[0, c]) for c, cu in enumerate(cols)]
    stores = [pltpu.make_async_copy(ubuf.at[:, cu], up_hbm.at[:, cu], sem.at[1, c]) for c, cu in enumerate(cols)]
    for cp in loads:
        cp.start()
    w = mix_in[...]
    diag = lax.broadcasted_iota(jnp.int32, w.shape, 0) == lax.broadcasted_iota(jnp.int32, w.shape, 1)
    mix_ref[...] = jnp.sum(jnp.where(diag, w, 0.0), axis=0)[:NUM_TASKS]
    down = lax.dot_general(tsum_in[...], ad_in[...], (((0,), (0,)), ((), ())), precision=lax.Precision.HIGHEST,
                           preferred_element_type=F32)
    dbuf[...] = down[:160]
    put = pltpu.make_async_copy(dbuf, down_hbm, sem.at[0, 4])
    put.start()
    for a, b in zip(loads, stores):
        a.wait()
        b.start()
    for cp in stores:
        cp.wait()
    put.wait()


def solution(mesh):
    def local_step(tok_rows, w_up, w_down, heads, label_rows):
        hc = jnp.transpose(heads, (0, 2, 1))
        vmem = pl.BlockSpec(memory_space=pltpu.VMEM)
        hbm = pl.BlockSpec(memory_space=pl.ANY)
        sds = jax.ShapeDtypeStruct
        dma = pltpu.SemaphoreType.DMA
        outs = pl.pallas_call(
            kernel,
            out_shape=(
                sds((NUM_TASKS, 128), F32),
                sds((40, HID), F32),
                sds((NUM_TASKS, 256), F32),
                sds((NUM_TASKS, DIM), F32),
                sds((NBLK, NTB, TB, CW), BF16),
                sds((TOK, DIM), BF16),
            ),
            in_specs=[hbm, hbm, hbm, vmem, vmem],
            out_specs=(vmem, hbm, vmem, vmem, hbm, hbm),
            scratch_shapes=[
                pltpu.VMEM((4, TB, DIM), BF16),
                pltpu.VMEM((DIM, HALF), BF16),
                pltpu.VMEM((2, 2, 4 * ROWS, PAIR_TOK), BF16),
                pltpu.VMEM((20, TB, CW), BF16),
                pltpu.VMEM((NTB, TB, CW), BF16),
                pltpu.VMEM((NTB, TB, CW), BF16),
                pltpu.VMEM((TB, 4 * TB), BF16),
                pltpu.VMEM((NUM_TASKS, TOK), F32),
                pltpu.VMEM((HALF, 128), BF16),
                pltpu.VMEM((NUM_TASKS, HALF), F32),
                pltpu.VMEM((DIM, 128), BF16),
                pltpu.VMEM((NUM_TASKS, PAIR_TOK), F32),
                pltpu.VMEM((NUM_TASKS, PAIR_TOK), F32),
                pltpu.VMEM((NUM_TASKS, TOK), jnp.int32),
                pltpu.VMEM((32, PAIR_TOK), BF16),
                pltpu.VMEM((NUM_TASKS, HALF), F32),
                pltpu.VMEM((NUM_CHIPS, NUM_TASKS, 256), F32),
                pltpu.VMEM((NUM_CHIPS, NUM_TASKS, 256), F32),
                pltpu.VMEM((NUM_CHIPS, NUM_TASKS, 128), F32),
                pltpu.VMEM((NUNIT, 2, 2, 2, 2, ROWS, UW), F32),
                pltpu.VMEM((NUNIT, 2, 2, 2, ROWS, UW), F32),
                pltpu.VMEM((NUNIT, 2, 2, ROWS, UW), F32),
                pltpu.VMEM((NUNIT, 2, ROWS, UW), F32),
                pltpu.VMEM((NUNIT, ROWS, UW), F32),
                dma((25,)), dma((5,)), dma((4,)), dma((2, NBLK)), dma((2,)),
                dma((3,)), dma((3,)), dma((15,)), dma((15,)), dma((16,)), dma((16,)),
                dma((5, NUNIT)), dma((5, NUNIT)), dma((NUNIT,)), dma((NUNIT,)), dma((NUNIT,)),
            ],
            compiler_params=pltpu.CompilerParams(
                collective_id=0, has_side_effects=True, vmem_limit_bytes=67043328),
        )(tok_rows, w_up, w_down, hc, label_rows)
        return pl.pallas_call(
            place,
            out_shape=(sds((NUM_TASKS,), F32), sds((40, HID), F32), sds((160, DIM), F32)),
            in_specs=[vmem, hbm, vmem, vmem],
            out_specs=(vmem, hbm, hbm),
            scratch_shapes=[pltpu.VMEM((40, HID), F32), pltpu.VMEM((160, DIM), F32), dma((2, 5))],
        )(*outs[:4])

    return jax.shard_map(
        local_step, mesh=mesh, in_specs=(P('data', None), P(), P(), P(), P(None, 'data')),
        out_specs=(P(), P('data', None), P('data', None)), check_vma=False)
```

time: 181 us -> 173 us (0.956)
  Pallas kernels: 178 us -> 172 us
    pallas_call x1, Pallas kernels: 175 us -> 168 us  [local_step(): pl.pallas_call(kernel, out_shape=(sds((NUM_TASKS, 128), F32), sds((40, HI...]
where the time goes in v3:
time: 173 us
  Pallas kernels  172 us (99%)
    pallas_call x1, Pallas kernels, local_step(): pl.pallas_call(kernel, out_shape=(sds((NUM_TASKS, 128), F32), sds((40, HI...  168 us
    pallas_call x1, Pallas kernels, local_step(): pl.pallas_call(place, out_shape=(sds((NUM_TASKS,), F32), sds((40, HID), F...  3.76 us

profile of v3, /device:TPU:0, one launch (start us, length us, event | category | flops | bytes accessed | tf_op | source)
XLA Modules:
  0.0 172.6 jit_solution(4473524735897675879)
XLA Ops:
  0.6 168.1 %shard_map.76 = (f32[8,128]{1,0:T(8,128)}, f32[40,5120]{1,0:T(8,128)}, f32[8,256]{1,0:T(8,128)}, f32[8,1280]{1,0:T(8,128)}, bf16[10,8,512,256]{3,2,1,0:T(8,128)(2,1)}, /*index=5*/bf16[2048,1280]{1,0:T(8,128)(2,1)}) custom-call(bf16[2048,1280]{1,0:T(8,128)(2,1)} %x_hbm.1, bf16[1280,5120]{1,0:T(8,128)(2,1)} %w1_hbm.1, bf16[5120,1280]{1,0:T(8,128)(2,1)} %w2_hbm.1, ...), custom_call_target="tpu_custom_call" | custom-call | tf_op jit(solution)/shard_map/pallas_call | solution.py:530
  168.7 3.8 %shard_map.77 = (f32[8]{0:T(128)}, f32[40,5120]{1,0:T(8,128)}, f32[160,1280]{1,0:T(8,128)}) custom-call(f32[8,128]{1,0:T(8,128)} %get-tuple-element.7.mix_in, f32[40,5120]{1,0:T(8,128)} %get-tuple-element.8.up_in, f32[8,256]{1,0:T(8,128)} %get-tuple-element.9.tsum_in, f32[8,1280]{1,0:T(8,128)} %get-tuple-element.10.ad_in), custom_call_target="tpu_custom_call" | custom-call | tf_op jit(solution)/shard_map/pallas_call | solution.py:574

commit v4 on v3

--- a/solution.py
+++ b/solution.py
@@ -209,12 +209,11 @@
     finish_prev(1, block_col(7))
     own = pl.ds(pl.multiple_of(core * TOK, TOK), TOK)
     st[:, own] += stx[...]
+    st_pair = remote(st, st_in, pair_s.at[2], pair_r.at[2], sib)
+    st_pair.start()
     for par in range(2):
         for nb in range(NBLK):
             a_store(par, nb, 0).wait()
-
-    st_pair = remote(st, st_in, pair_s.at[2], pair_r.at[2], sib)
-    st_pair.start()
 
     def a_load(j):
         return pltpu.make_async_copy(
@@ -474,8 +473,8 @@
     tsum_ref[...] = tsum
     ad_ref[...] = diff * wcol
 
-    for b in range(NBLK + 2, NBLK + PLAN[-1][2]):
-        late(b)
+    late(NBLK + 2)
+    late(NBLK + 3)
 
     x_pair.wait_send()
     lab_pair.wait_send()
@@ -489,13 +488,22 @@
 
     def drain(j, carry):
         for h in range(2):
-            for s in range(5):
+            for s in range(4):
                 copy(j, h, s).wait_send()
+        return carry
+
+    def drain_out(j, carry):
+        for h in range(2):
+            copy(j, h, 4).wait_send()
             out_local(2 * j + h).wait()
             out_pair(2 * j + h).wait()
         return carry
 
     lax.fori_loop(0, NBLK, drain, 0)
+    lax.fori_loop(0, NBLK - 3, drain_out, 0)
+    late(NBLK + 4)
+    late(NBLK + 5)
+    lax.fori_loop(NBLK - 3, NBLK, drain_out, 0)
 
 
 def place(mix_in, up_in, tsum_in, ad_in, mix_ref, up_hbm, down_hbm, ubuf, dbuf, sem):

time: 173 us -> 172 us (level)
  no operation moved by 1% of the time
where the time goes in v4:
time: 172 us
  Pallas kernels  171 us (99%)
    pallas_call x1, Pallas kernels, local_step(): pl.pallas_call(kernel, out_shape=(sds((NUM_TASKS, 128), F32), sds((40, HI...  167 us
    pallas_call x1, Pallas kernels, local_step(): pl.pallas_call(place, out_shape=(sds((NUM_TASKS,), F32), sds((40, HID), F...  3.76 us

profile of v4, /device:TPU:0, one launch (start us, length us, event | category | flops | bytes accessed | tf_op | source)
XLA Modules:
  0.0 171.8 jit_solution(5139918538112364109)
XLA Ops:
  0.6 167.2 %shard_map.76 = (f32[8,128]{1,0:T(8,128)}, f32[40,5120]{1,0:T(8,128)}, f32[8,256]{1,0:T(8,128)}, f32[8,1280]{1,0:T(8,128)}, bf16[10,8,512,256]{3,2,1,0:T(8,128)(2,1)}, /*index=5*/bf16[2048,1280]{1,0:T(8,128)(2,1)}) custom-call(bf16[2048,1280]{1,0:T(8,128)(2,1)} %x_hbm.1, bf16[1280,5120]{1,0:T(8,128)(2,1)} %w1_hbm.1, bf16[5120,1280]{1,0:T(8,128)(2,1)} %w2_hbm.1, ...), custom_call_target="tpu_custom_call" | custom-call | tf_op jit(solution)/shard_map/pallas_call | solution.py:538
  167.8 3.8 %shard_map.77 = (f32[8]{0:T(128)}, f32[40,5120]{1,0:T(8,128)}, f32[160,1280]{1,0:T(8,128)}) custom-call(f32[8,128]{1,0:T(8,128)} %get-tuple-element.7.mix_in, f32[40,5120]{1,0:T(8,128)} %get-tuple-element.8.up_in, f32[8,256]{1,0:T(8,128)} %get-tuple-element.9.tsum_in, f32[8,1280]{1,0:T(8,128)} %get-tuple-element.10.ad_in), custom_call_target="tpu_custom_call" | custom-call | tf_op jit(solution)/shard_map/pallas_call | solution.py:582
